TPU v7x, 16 devices: a whole 2x2x2 slice. The times are simulated.
16 devices in a mesh: tp: 2 (over z), dp: 8 (over y, x, core).
Axes of the slice: x: 2, y: 2, z: 2, core: 2. Of those that a mesh axis runs over, the one named last changes fastest.
Arguments:
- hidden: bfloat16 [8192, 2048], P('dp')
- norm_w: bfloat16 [2048], replicated
- emb_table: bfloat16 [49152, 2048], P('tp')
- teacher: bfloat16 [8192, 49152], P('dp', 'tp')
- loss_mask: int32 [8192], P('dp')
Outputs:
- output 1: float32 [], replicated
- output 2: bfloat16 [8192, 2048], P('dp')
- output 3: float32 [49152, 2048], P('tp', 'dp')
- output 4: float32 [2048], replicated
All inputs are finite; a program needn't handle non-finite values.
Results may differ from a plain program's by a relative error of at most 0.00103826.
Values sent between devices are 32-bit elements.
A program may use at most 1 GiB of HBM per device.

v0:
```python
import jax
import jax.numpy as jnp
from jax import lax
from jax.sharding import PartitionSpec as P

SOFT_CAP = 30.0
NORM_EPS = 1e-6


def rms_norm(hid_f32, scale_f32):
    inv_rms = lax.rsqrt(jnp.mean(hid_f32 * hid_f32, axis=-1, keepdims=True) + NORM_EPS)
    return hid_f32 * inv_rms * (1.0 + scale_f32)


def solution(mesh):
    def device_fn(hid_loc, norm_w, emb_loc, teach_loc, mask_loc):
        mask_f32 = mask_loc.astype(jnp.float32)
        tok_count = lax.psum(jnp.sum(mask_f32), 'dp')
        weight = mask_f32 / tok_count
        normed_f32, norm_pull = jax.vjp(rms_norm, hid_loc.astype(jnp.float32), norm_w.astype(jnp.float32))
        normed = normed_f32.astype(jnp.bfloat16)
        raw_logit = jnp.einsum('nd,vd->nv', normed, emb_loc, preferred_element_type=jnp.float32)
        tanh_val = jnp.tanh(raw_logit / SOFT_CAP)
        capped = SOFT_CAP * tanh_val
        teach_f32 = teach_loc.astype(jnp.float32)
        maxima = lax.pmax(jnp.stack([jnp.max(capped, axis=-1), jnp.max(teach_f32, axis=-1)], axis=-1), 'tp')
        stu_exp = jnp.exp(capped - maxima[:, 0:1])
        tea_exp = jnp.exp(teach_f32 - maxima[:, 1:2])
        local_sums = jnp.stack([jnp.sum(stu_exp, axis=-1), jnp.sum(tea_exp, axis=-1), jnp.sum(tea_exp * (teach_f32 - capped), axis=-1)], axis=-1)
        totals = lax.psum(local_sums, 'tp')
        lse_stu = maxima[:, 0] + jnp.log(totals[:, 0])
        lse_tea = maxima[:, 1] + jnp.log(totals[:, 1])
        kl_tok = totals[:, 2] / totals[:, 1] - lse_tea + lse_stu
        loss_val = lax.psum(jnp.sum(weight * kl_tok), 'dp')
        prob_diff = stu_exp / totals[:, 0:1] - tea_exp / totals[:, 1:2]
        d_raw = (prob_diff * weight[:, None] * (1.0 - tanh_val * tanh_val)).astype(jnp.bfloat16)
        grad_normed = lax.psum(jnp.dot(d_raw, emb_loc, preferred_element_type=jnp.float32), 'tp')
        emb_part = jnp.einsum('nv,nd->vd', d_raw, normed, preferred_element_type=jnp.float32)
        grad_emb = lax.psum_scatter(emb_part, 'dp', scatter_dimension=1, tiled=True)
        grad_hid, grad_scale = norm_pull(grad_normed)
        grad_w = lax.psum(grad_scale, 'dp')
        return loss_val, grad_hid.astype(jnp.bfloat16), grad_emb, grad_w

    return jax.shard_map(device_fn, mesh=mesh, in_specs=(P('dp', None), P(None), P('tp', None), P('dp', 'tp'), P('dp')), out_specs=(P(), P('dp', None), P('tp', 'dp'), P(None)), check_vma=False)
```

profile of v0, /device:TPU:0, one launch (start us, length us, event | category | flops | bytes accessed | tf_op | source)
XLA Modules:
  0.0 1609.8 jit_solution(7060595784179449416)
XLA Ops:
  8.0 0.0 copy-start.8
  8.0 0.0 all-reduce.3.cloned.1.call-start
  8.1 1.3 convert_reduce_fusion
  9.3 16.0 psum.35
  25.4 16.0 reduce_max.26
  41.4 0.6 reduce_max.29
  42.0 3.1 fusion.17
  45.0 0.0 copy-start.4
  45.1 0.6 copy-done.4
  45.6 0.0 copy-done.8
  45.7 0.0 copy-start
  45.7 0.0 copy-start.6
  45.7 115.6 %fusion.11 = (f32[1024]{0:T(1024)S(1)}, f32[1024,24576]{1,0:T(8,128)}) fusion(bf16[24576,2048]{1,0:T(8,128)(2,1)} %param.7, bf16[1024,2048]{1,0:T(8,128)(2,1)} %param.5, f32[2048]{0:T(1024)S(1)} %convert_add_fusion, f32[1024]{0:T(1024)S(1)} %fusion.23), kind=kOutput, calls=%fused_computation.15 | convolution fusion | flops 103163101184 | bytes 205537280 | tf_op jit(solution)/shard_map/nd,vd->nv/dot_general | solution.py:22
  161.3 0.0 copy-done.2
  161.3 0.0 copy-done
  161.3 0.0 copy-done.6
  161.4 5.0 pmax.7
  166.4 0.0 copy-start.7
  166.4 79.2 %fusion.10 = (f32[1024]{0:T(1024)S(1)}, f32[1024]{0:T(1024)S(1)}, f32[1024]{0:T(1024)S(1)}) fusion(f32[1024,24576]{1,0:T(8,128)} %get-tuple-element.19, f32[1024]{0:T(1024)S(1)} %bitcast.19, f32[1024]{0:T(1024)S(1)} %bitcast.16, bf16[1024,24576]{1,0:T(8,128)(2,1)} %param.8), kind=kLoop, calls=%fused_computation.14 | loop fusion | flops 251655168 | bytes 151015424 | tf_op jit(solution)/shard_map/reduce_sum | solution.py:29
  245.6 8.2 psum.36
  253.9 1.3 multiply_reduce_fusion
  255.2 69.3 %fusion.8 = bf16[1024,24576]{1,0:T(8,128)(2,1)} fusion(bf16[1024,24576]{1,0:T(8,128)(2,1)} %param.8, f32[1024,24576]{1,0:T(8,128)} %get-tuple-element.19, f32[1024]{0:T(1024)S(1)} %get-tuple-element.12, f32[1024]{0:T(1024)S(1)} %bitcast.25, f32[1024]{0:T(1024)S(1)} %bitcast.23, f32[1024]{0:T(1024)S(1)} %bitcast.18, f32[1024]{0:T(1024)S(1)} %bitcast.21), kind=kLoop, calls=%fused_computation.12 | loop fusion | flops 327155712 | bytes 201347072 | tf_op jit(solution)/shard_map/convert_element_type | solution.py:36
  324.5 114.9 %fusion.26 = f32[1024,2048]{1,0:T(8,128)} fusion(bf16[1024,24576]{1,0:T(8,128)(2,1)} %fusion.8, bf16[24576,2048]{1,0:T(8,128)(2,1)} %param.7), kind=kOutput, calls=%fused_computation.41 | convolution fusion | flops 103079215104 | bytes 159383552 | tf_op jit(solution)/shard_map/dot_general | solution.py:37
  439.4 0.0 all-reduce.3.cloned.1.call-update
  439.4 0.0 reduce-scatter.2.cloned.1.call-start
  439.5 119.5 %fusion.19 = f32[24576,2048]{1,0:T(8,128)} fusion(bf16[1024,24576]{1,0:T(8,128)(2,1)} %fusion.8, bf16[1024,2048]{1,0:T(8,128)(2,1)} %param.5, f32[2048]{0:T(1024)S(1)} %copy-done.1, f32[1024]{0:T(1024)S(1)} %copy-done.3), kind=kOutput, calls=%fused_computation.28 | convolution fusion | flops 103087603712 | bytes 255864832 | tf_op jit(solution)/shard_map/nv,nd->vd/dot_general | solution.py:38
  558.9 0.0 reduce-scatter.2.cloned.1.call-update
  558.9 72.8 %all-reduce.3.cloned.1.call-done = f32[1024,2048]{1,0:T(8,128)} async-done(((f32[1024,2048]{1,0:T(8,128)}), f32[1024,2048]{1,0:T(8,128)}) %all-reduce.3.cloned.1.call-update) | async-done | bytes 8388624 | tf_op jit(solution)/shard_map/psum | solution.py:37
  631.7 6.1 fusion.15
  637.8 14.5 all-reduce
  652.4 6.9 fusion.16
  659.3 943.1 %reduce-scatter.2.cloned.1.call-done = f32[24576,256]{1,0:T(8,128)} async-done(((f32[24576,2048]{1,0:T(8,128)}), f32[24576,256]{1,0:T(8,128)}) %reduce-scatter.2.cloned.1.call-update) | async-done | bytes 25165840 | tf_op jit(solution)/shard_map/reduce_scatter | solution.py:39
  (15 shorter events, 0.1 us)
Async XLA Ops:
  8.0 37.6 %copy-start.8 = (bf16[2048]{0:T(1024)(128)(2,1)S(1)}, bf16[2048]{0:T(1024)(128)(2,1)}, u32[]{:S(2)}) copy-start(bf16[2048]{0:T(1024)(128)(2,1)} %param.6) | copy-start | bytes 12292
  8.0 623.7 %all-reduce.3.cloned.1.call-start = ((), (), s32[]{:S(2)}) async-start(), calls=%async_computation.1 | async-start | bytes 16777216 | tf_op jit(solution)/shard_map/psum | solution.py:37
  45.0 0.6 copy-start.4
  45.6 115.7 %copy-start.2 = (f32[1024]{0:T(1024)}, f32[1024]{0:T(1024)S(1)}, u32[]{:S(2)}) copy-start(f32[1024]{0:T(1024)S(1)} %fusion.23) | copy-start | bytes 12292
  45.7 115.7 %copy-start = (f32[2048]{0:T(1024)}, f32[2048]{0:T(1024)S(1)}, u32[]{:S(2)}) copy-start(f32[2048]{0:T(1024)S(1)} %convert_add_fusion) | copy-start | bytes 24580
  45.7 115.7 %copy-start.6 = (f32[1024]{0:T(1024)S(1)}, f32[1024]{0:T(1024)}, u32[]{:S(2)}) copy-start(f32[1024]{0:T(1024)} %reduce_max.29) | copy-start | bytes 12292
  166.4 87.5 %copy-start.7 = (s32[1024]{0:T(1024)S(1)}, s32[1024]{0:T(1024)}, u32[]{:S(2)}) copy-start(s32[1024]{0:T(1024)} %param.9) | copy-start | bytes 12292
  324.5 115.0 %copy-start.1 = (f32[2048]{0:T(1024)S(1)}, f32[2048]{0:T(1024)}, u32[]{:S(2)}) copy-start(f32[2048]{0:T(1024)} %copy-done) | copy-start | bytes 24580
  324.5 115.0 %copy-start.3 = (f32[1024]{0:T(1024)S(1)}, f32[1024]{0:T(1024)}, u32[]{:S(2)}) copy-start(f32[1024]{0:T(1024)} %copy-done.2) | copy-start | bytes 12292
  439.4 1163.0 %reduce-scatter.2.cloned.1.call-start = ((), (), s32[]{:S(2)}) async-start(), calls=%async_computation.2 | async-start | bytes 226492416 | tf_op jit(solution)/shard_map/reduce_scatter | solution.py:39
  558.9 93.5 %copy-start.5 = (f32[1024]{0:T(1024)S(1)}, f32[1024]{0:T(1024)}, u32[]{:S(2)}) copy-start(f32[1024]{0:T(1024)} %copy-done.4) | copy-start | bytes 12292
Sparse Core Ops, SparseCore 0:
  439.5 192.1 all-reduce.2
Sparse Core Ops, SparseCore 1:
  559.0 1043.3 reduce-scatter.1
where the time goes:
time: 1610 us
  waiting for transfers between devices  1020 us (63%)
  matrix products  350 us (22%)
  other arithmetic  184 us (11%)
  blocking collectives  43.8 us (3%)
    reduce_scatter x1, waiting for transfers between devices, device_fn(): grad_emb = lax.psum_scatter(emb_part, 'dp', scatter_dimension=1, tiled=True)  943 us
    dot_general x1, matrix products, device_fn(): jnp.einsum('nv,nd->vd', d_raw, normed, preferred_element_type=jnp.float32)  119 us
    dot_general x1, matrix products, device_fn(): jnp.einsum('nd,vd->nv', normed, emb_loc, preferred_element_type=jnp.float32)  116 us
    dot_general x1, matrix products, device_fn(): jnp.dot(d_raw, emb_loc, preferred_element_type=jnp.float32)  115 us
    reduce_sum x1, other arithmetic, device_fn(): jnp.sum(stu_exp, axis=-1)  79.2 us
    psum x1, waiting for transfers between devices, device_fn(): lax.psum(jnp.dot(d_raw, emb_loc, preferred_element_type=jnp.float32), 'tp')  72.8 us
    convert_element_type x1, other arithmetic, device_fn(): (prob_diff * weight[:, None] * (1.0 - tanh_val * tanh_val)).astype(jnp.bf...  69.3 us
  transfers between devices with their start and end apart: 2, of which 2 were waited for; matrix products, arithmetic and copies ran while one was open for 8% of the time, Pallas kernels for 0%

commit v1 on v0

v1 whole, which is shorter than its diff:
```python
import functools

import jax
import jax.numpy as jnp
from jax import lax
from jax.experimental import pallas as pl
from jax.experimental.pallas import tpu as pltpu
from jax.sharding import PartitionSpec as P

SOFT_CAP = 30.0
NORM_EPS = 1e-6
LANES = 128
SUB = 256
FWD_SUB = 512
NSLOT = 8
MESH = pl.DeviceIdType.MESH
NT = (((1,), (1,)), ((), ()))


def rms_norm(hid_f32, scale_f32):
    inv_rms = lax.rsqrt(jnp.mean(hid_f32 * hid_f32, axis=-1, keepdims=True) + NORM_EPS)
    return hid_f32 * inv_rms * (1.0 + scale_f32)


def stats_kernel(steps, g_ref, e_ref, ta_ref, tb_ref, out_ref, ra, rb, mx, st, su, ss):
    i = pl.program_id(0)
    sub = ra.shape[1]

    @pl.when(i == 0)
    def _():
        mx[...] = jnp.full_like(mx, -jnp.inf)
        for ref in (st, su, ss):
            ref[...] = jnp.zeros_like(ref)

    def stats(pairs, rows):
        parts = [(r, t, slice(c * LANES, (c + 1) * LANES)) for r, t in pairs for c in range(sub // LANES)]
        old = mx[rows]
        new = old
        for _, t_ref, cols in parts:
            new = jnp.maximum(new, t_ref[rows, cols].astype(jnp.float32))
        keep = jnp.exp(old - new)
        mx[rows] = new
        t_sum = st[rows] * keep
        u_sum = su[rows] * keep
        s_sum = ss[rows]
        for r_ref, t_ref, cols in parts:
            z = SOFT_CAP * jnp.tanh(r_ref[rows, cols] * (1.0 / SOFT_CAP))
            s_sum += jnp.exp(z)
            t = t_ref[rows, cols].astype(jnp.float32)
            te = jnp.exp(t - new)
            t_sum += te
            u_sum += te * (t - z)
        st[rows] = t_sum
        su[rows] = u_sum
        ss[rows] = s_sum

    n_chunk = 4
    m = g_ref.shape[0] // n_chunk
    for q in range(n_chunk):
        rows = slice(q * m, (q + 1) * m)
        r = lax.dot_general(g_ref[rows], e_ref[...], NT, preferred_element_type=jnp.float32)
        ra[rows] = r[:, 0:sub]
        rb[rows] = r[:, sub:]
        stats([(ra, ta_ref), (rb, tb_ref)], rows)

    @pl.when(i == steps - 1)
    def _():
        top = jnp.max(mx[...], axis=1, keepdims=True)
        keep = jnp.exp(mx[...] - top)
        out_ref[0] = jnp.broadcast_to(top, mx.shape)
        out_ref[1] = jnp.broadcast_to(jnp.sum(st[...] * keep, axis=1, keepdims=True), mx.shape)
        out_ref[2] = jnp.broadcast_to(jnp.sum(su[...] * keep, axis=1, keepdims=True), mx.shape)
        out_ref[3] = jnp.broadcast_to(jnp.sum(ss[...], axis=1, keepdims=True), mx.shape)


def forward_stats(g, emb, teach):
    rows, width = g.shape
    vocab = emb.shape[0]
    steps = vocab // (2 * FWD_SUB)
    return pl.pallas_call(
        functools.partial(stats_kernel, steps),
        grid=(steps,),
        out_shape=jax.ShapeDtypeStruct((4, rows, LANES), jnp.float32),
        in_specs=[
            pl.BlockSpec((rows, width), lambda i: (0, 0), pipeline_mode=pl.Buffered(1)),
            pl.BlockSpec((2 * FWD_SUB, width), lambda i: (i, 0)),
            pl.BlockSpec((rows, FWD_SUB), lambda i: (0, 2 * i)),
            pl.BlockSpec((rows, FWD_SUB), lambda i: (0, 2 * i + 1)),
        ],
        out_specs=pl.BlockSpec((4, rows, LANES), lambda i: (0, 0, 0)),
        scratch_shapes=[pltpu.VMEM((rows, FWD_SUB), jnp.float32)] * 2 + [pltpu.VMEM((rows, LANES), jnp.float32)] * 4,
        compiler_params=pltpu.CompilerParams(
            dimension_semantics=("arbitrary",), vmem_limit_bytes=60 * 1024 * 1024
        ),
        cost_estimate=pl.CostEstimate(
            flops=2 * rows * width * vocab, bytes_accessed=2 * vocab * (width + rows), transcendentals=3 * rows * vocab
        ),
        name="fwd_stats",
    )(g, emb, teach, teach)


def grad_kernel(blocks, base, g_ref, x_ref, w_ref, row_ref, mine_ref, e_ref, t_ref, ex_ref, tx_ref,
                de_ref, dh_ref, tot_ref, dhs, wrow, misc_in, comb, comb_in, drb, drx, drt, dgacc, dgin, own, snd, d_in, x2, y2, x3, y3,
                d_ss, d_rs, x2_ss, x2_rs, y2_ss, y2_rs, x3_ss, x3_rs, y3_ss, y3_rs, o_sem, z_ss, z_rs, dh_sem, x_sem, m_ss, m_rs, c_ss, c_rs):
    i = pl.program_id(0)
    dp = lax.axis_index("dp")
    tp = lax.axis_index("tp")
    core = lax.rem(dp, 2)
    chip = dp // 2
    xi = lax.rem(chip, 2)
    yi = chip // 2
    chips = (chip, chip + 1 - 2 * xi, 3 - chip, chip + 2 - 4 * yi)
    sib = {"dp": dp + 1 - 2 * core}
    xn = {"dp": chips[1] * 2 + core}
    yn = {"dp": chips[3] * 2 + core}
    zn = {"tp": 1 - tp}
    half = SUB // 2
    zrows = dgacc.shape[0] // z_ss.shape[0]

    def remote(src, dst, ss, rs, to):
        return pltpu.make_async_remote_copy(src_ref=src, dst_ref=dst, send_sem=ss, recv_sem=rs, device_id=to, device_id_type=MESH)

    def d_copy(k):
        s = lax.rem(k, 2)
        return remote(snd, d_in.at[s], d_ss, d_rs.at[s], sib)

    def x2_copy(k):
        s, r = lax.rem(k, NSLOT), lax.rem(k, x2.shape[0])
        return remote(own.at[s, pl.ds(1, 2), pl.ds(0, half)], x2.at[r], x2_ss.at[s], x2_rs.at[r], xn)

    def y2_copy(k):
        s, r = lax.rem(k, NSLOT), lax.rem(k, y2.shape[0])
        return remote(own.at[s, pl.ds(2, 2), pl.ds(half, half)], y2.at[r], y2_ss.at[s], y2_rs.at[r], yn)

    def y3_copy(k):
        s = lax.rem(k, NSLOT)
        return remote(own.at[s, 3, pl.ds(0, half)], y3.at[s], y3_ss.at[s], y3_rs.at[s], yn)

    def x3_copy(k):
        s = lax.rem(k, NSLOT)
        return remote(own.at[s, 1, pl.ds(half, half)], x3.at[s], x3_ss.at[s], x3_rs.at[s], xn)

    def out_copy(k):
        s = lax.rem(k, NSLOT)
        return pltpu.make_async_copy(own.at[s, 0], de_ref.at[pl.ds(pl.multiple_of(k * SUB, SUB), SUB)], o_sem.at[s])

    def z_copy(q):
        rows = pl.ds(q * zrows, zrows)
        return remote(dgacc.at[rows], dgin.at[rows], z_ss.at[q], z_rs.at[q], zn)

    n_dp = misc_in.shape[0]

    def to_all(src, dst, ss, rs, j, arriving):
        slot = lax.rem(dp + (n_dp - j if arriving else 0), n_dp)
        return remote(src, dst.at[slot], ss.at[j], rs.at[j], {"dp": lax.rem(dp + j, n_dp)})

    @pl.when(i == 0)
    def _():
        barrier = pltpu.get_barrier_semaphore()
        for j in range(1, n_dp):
            pl.semaphore_signal(barrier, inc=1, device_id={"dp": lax.rem(dp + j, n_dp)}, device_id_type=MESH)
        pl.semaphore_signal(barrier, inc=1, device_id=zn, device_id_type=MESH)
        pl.semaphore_wait(barrier, n_dp)
        for j in range(1, n_dp):
            to_all(mine_ref, misc_in, m_ss, m_rs, j, False).start()
        dgacc[...] = jnp.zeros_like(dgacc)
        misc_in[dp] = mine_ref[...]
        for j in range(1, n_dp):
            to_all(mine_ref, misc_in, m_ss, m_rs, j, False).wait_send()
            to_all(mine_ref, misc_in, m_ss, m_rs, j, True).wait_recv()
        total = misc_in[0]
        for d in range(1, n_dp):
            total += misc_in[d]
        wrow[...] = row_ref[2] / total[0:1, :]
        tot_ref[16:24, :] = jnp.broadcast_to(total[1:2, :] / total[0:1, :], (8, LANES))

    def make_dr(er, tr, dr):
        raw = lax.dot_general(g_ref[...], er[...], NT, preferred_element_type=jnp.float32)
        for c in range(SUB // LANES):
            cols = slice(c * LANES, (c + 1) * LANES)
            th = jnp.tanh(raw[:, cols] * (1.0 / SOFT_CAP))
            ps = jnp.exp(SOFT_CAP * th - row_ref[0])
            pt = jnp.exp(tr[:, cols].astype(jnp.float32) - row_ref[1])
            dr[:, cols] = ((ps - pt) * wrow[...] * (1.0 - th * th)).astype(jnp.bfloat16)

    def add_dg(er, dr):
        for c in range(dgacc.shape[1] // 512):
            cols = slice(c * 512, (c + 1) * 512)
            dgacc[:, cols] += jnp.dot(dr[...], er[:, cols], preferred_element_type=jnp.float32)

    def second_stage():
        k = i - 1
        s = lax.rem(k, NSLOT)
        d_copy(k).wait()
        own[s] += d_in[lax.rem(k, 2)]
        x2_copy(k).start()
        y2_copy(k).start()

    @pl.when(i == 1)
    def _():
        second_stage()

    @pl.when((i >= 3) & (i < blocks + 3))
    def _():
        k = i - 3
        s, r = lax.rem(k, NSLOT), lax.rem(k, x2.shape[0])
        x2_copy(k).wait_recv()
        own[s, 0, 0:half] += x2[r, 0]
        own[s, 3, 0:half] += x2[r, 1]
        y3_copy(k).start()
        y2_copy(k).wait_recv()
        own[s, 1, half:] += y2[r, 0]
        x3_copy(k).start()
        own[s, 0, half:] += y2[r, 1]

    @pl.when(i < blocks)
    def _():
        make_dr(e_ref, t_ref, drb)
        drt[...] = drb[...].T

    @pl.when(i == base)
    def _():
        for q in range(z_ss.shape[0]):
            z_copy(q).start()
        pltpu.make_async_copy(x_ref, dhs, x_sem).start()

    @pl.when((i >= 2) & (i < blocks + 1))
    def _():
        second_stage()

    @pl.when(i < blocks)
    def _():
        s = lax.rem(i, NSLOT)
        for j in range(4):
            cols = pl.ds(pl.multiple_of((2 * chips[j] + 1 - core) * SUB, SUB), SUB)
            snd[j] = jnp.dot(drt[...], g_ref[:, cols], preferred_element_type=jnp.float32)
        d_copy(i).start()
        for j in range(4):
            cols = pl.ds(pl.multiple_of((2 * chips[j] + core) * SUB, SUB), SUB)
            own[s, j] = jnp.dot(drt[...], g_ref[:, cols], preferred_element_type=jnp.float32)

    @pl.when(i < base)
    def _():
        add_dg(e_ref, drb)

    @pl.when((i < base) & (lax.rem(i, 2) == 0))
    def _():
        make_dr(ex_ref, tx_ref, drx)

    @pl.when((i < base) & (lax.rem(i, 2) == 1))
    def _():
        add_dg(ex_ref, drx)

    @pl.when((i >= 5) & (i < blocks + 5))
    def _():
        k = i - 5
        s = lax.rem(k, NSLOT)
        y3_copy(k).wait_recv()
        own[s, 0, 0:half] += y3[s]
        x3_copy(k).wait_recv()
        own[s, 0, half:] += x3[s]
        out_copy(k).start()

    @pl.when(i >= 6)
    def _():
        k = i - 6
        x2_copy(k).wait_send()
        y2_copy(k).wait_send()
        x3_copy(k).wait_send()
        y3_copy(k).wait_send()
        out_copy(k).wait()

    @pl.when(i == blocks - 5)
    def _():
        for q in range(z_ss.shape[0]):
            z_copy(q).wait()
        pltpu.make_async_copy(x_ref, dhs, x_sem).wait()
        gain = 1.0 + w_ref[...]
        part = 128
        comb[...] = jnp.zeros_like(comb)

        @pl.loop(0, dgacc.shape[0] // part)
        def _(q):
            rows = pl.ds(pl.multiple_of(q * part, part), part)
            x = dhs[rows, :].astype(jnp.float32)
            dg = dgacc[rows, :] + dgin[rows, :]
            inv = lax.rsqrt(jnp.mean(x * x, axis=-1, keepdims=True) + NORM_EPS)
            dy = dg * gain
            dot = jnp.sum(dy * x, axis=-1, keepdims=True)
            dhs[rows, :] = (dy * inv - x * (dot * (inv * inv * inv) * (1.0 / x.shape[1]))).astype(jnp.bfloat16)
            dw = jnp.sum(dg * x * inv, axis=0, keepdims=True)
            for c in range(comb.shape[0]):
                comb[c:c + 1, :] += dw[:, c * LANES:(c + 1) * LANES]

        pltpu.make_async_copy(dhs, dh_ref, dh_sem).start()

    @pl.when(i == blocks - 4)
    def _():
        for j in range(1, n_dp):
            to_all(comb, comb_in, c_ss, c_rs, j, False).start()
        comb_in[dp] = comb[...]

    @pl.when(i == blocks + 5)
    def _():
        pltpu.make_async_copy(dhs, dh_ref, dh_sem).wait()
        for j in range(1, n_dp):
            to_all(comb, comb_in, c_ss, c_rs, j, False).wait_send()
            to_all(comb, comb_in, c_ss, c_rs, j, True).wait_recv()
        total = comb_in[0]
        for d in range(1, n_dp):
            total += comb_in[d]
        tot_ref[0:16, :] = total


def backward(g, hid, scale, row, mine, emb, teach, n_dp):
    rows, width = g.shape
    vocab = emb.shape[0]
    blocks = vocab // SUB
    base = blocks * 2 // 3
    last = blocks - 1

    def main(i):
        return jnp.minimum(i, last)

    def extra(i):
        return base + jnp.minimum(i // 2, blocks - base - 1)

    f32 = jnp.float32
    half = SUB // 2
    dma = pltpu.SemaphoreType.DMA
    return pl.pallas_call(
        functools.partial(grad_kernel, blocks, base),
        grid=(blocks + 6,),
        out_shape=(
            jax.ShapeDtypeStruct((vocab, SUB), f32),
            jax.ShapeDtypeStruct((rows, width), jnp.bfloat16),
            jax.ShapeDtypeStruct((width // LANES + 8, LANES), f32),
        ),
        in_specs=[
            pl.BlockSpec((rows, width), lambda i: (0, 0), pipeline_mode=pl.Buffered(1)),
            pl.BlockSpec(memory_space=pl.ANY),
            pl.BlockSpec((1, width), lambda i: (0, 0), pipeline_mode=pl.Buffered(1)),
            pl.BlockSpec((3, rows, LANES), lambda i: (0, 0, 0), pipeline_mode=pl.Buffered(1)),
            pl.BlockSpec((8, LANES), lambda i: (0, 0), pipeline_mode=pl.Buffered(1)),
            pl.BlockSpec((SUB, width), lambda i: (main(i), 0)),
            pl.BlockSpec((rows, SUB), lambda i: (0, main(i))),
            pl.BlockSpec((SUB, width), lambda i: (extra(i), 0)),
            pl.BlockSpec((rows, SUB), lambda i: (0, extra(i))),
        ],
        out_specs=(
            pl.BlockSpec(memory_space=pl.ANY),
            pl.BlockSpec(memory_space=pl.ANY),
            pl.BlockSpec((width // LANES + 8, LANES), lambda i: (0, 0)),
        ),
        scratch_shapes=[
            pltpu.VMEM((rows, width), jnp.bfloat16),
            pltpu.VMEM((rows, LANES), f32),
            pltpu.VMEM((n_dp, 8, LANES), f32),
            pltpu.VMEM((width // LANES, LANES), f32),
            pltpu.VMEM((n_dp, width // LANES, LANES), f32),
            pltpu.VMEM((rows, SUB), jnp.bfloat16),
            pltpu.VMEM((rows, SUB), jnp.bfloat16),
            pltpu.VMEM((SUB, rows), jnp.bfloat16),
            pltpu.VMEM((rows, width), f32),
            pltpu.VMEM((rows, width), f32),
            pltpu.VMEM((NSLOT, 4, SUB, SUB), f32),
            pltpu.VMEM((4, SUB, SUB), f32),
            pltpu.VMEM((2, 4, SUB, SUB), f32),
            pltpu.VMEM((4, 2, half, SUB), f32),
            pltpu.VMEM((4, 2, half, SUB), f32),
            pltpu.VMEM((NSLOT, half, SUB), f32),
            pltpu.VMEM((NSLOT, half, SUB), f32),
            dma, dma((2,)), dma((NSLOT,)), dma((4,)), dma((NSLOT,)), dma((4,)),
            dma((NSLOT,)), dma((NSLOT,)), dma((NSLOT,)), dma((NSLOT,)), dma((NSLOT,)), dma((4,)), dma((4,)), dma, dma,
            dma((n_dp,)), dma((n_dp,)), dma((n_dp,)), dma((n_dp,)),
        ],
        compiler_params=pltpu.CompilerParams(
            dimension_semantics=("arbitrary",), collective_id=0, has_side_effects=True, vmem_limit_bytes=62 * 1024 * 1024
        ),
        cost_estimate=pl.CostEstimate(
            flops=6 * rows * width * vocab, bytes_accessed=2 * vocab * (width + rows), transcendentals=3 * rows * vocab
        ),
        name="bwd_scatter",
    )(g, hid, scale, row, mine, emb, teach, emb, teach)


def solution(mesh):

    def device_fn(hid_loc, norm_w, emb_loc, teach_loc, mask_loc):
        mask_f32 = mask_loc.astype(jnp.float32)
        scale = norm_w.astype(jnp.float32)
        normed = rms_norm(hid_loc.astype(jnp.float32), scale).astype(jnp.bfloat16)
        part = forward_stats(normed, emb_loc, teach_loc)[:, :, 0]
        parts = lax.all_gather(part, "tp")
        top = jnp.max(parts[:, 0], axis=0)
        keep = jnp.exp(parts[:, 0] - top)
        tea_sum = jnp.sum(parts[:, 1] * keep, axis=0)
        cross = jnp.sum(parts[:, 2] * keep, axis=0)
        lse_tea = top + jnp.log(tea_sum)
        lse_stu = jnp.log(jnp.sum(parts[:, 3], axis=0))
        kl_tok = cross / tea_sum - lse_tea + lse_stu
        row = jnp.broadcast_to(jnp.stack([lse_stu, lse_tea, mask_f32])[:, :, None], (3, mask_f32.shape[0], LANES))
        sums = jnp.stack([jnp.sum(mask_f32), jnp.sum(mask_f32 * kl_tok)])
        mine = jnp.broadcast_to(jnp.pad(sums, (0, 6))[:, None], (8, LANES))
        grad_emb, grad_hid, total = backward(normed, hid_loc, scale[None, :], row, mine, emb_loc, teach_loc, mesh.shape["dp"])
        return total[-1, 0], grad_hid, grad_emb, total[:-8].reshape(-1)

    return jax.shard_map(device_fn, mesh=mesh, in_specs=(P('dp', None), P(None), P('tp', None), P('dp', 'tp'), P('dp')), out_specs=(P(), P('dp', None), P('tp', 'dp'), P(None)), check_vma=False)
```

time: 1610 us -> 1030 us (0.64)
  waiting for transfers between devices: 1020 us -> 0 us
  Pallas kernels: 0 us -> 985 us
  matrix products: 350 us -> 0 us
  other arithmetic: 184 us -> 13.1 us
  blocking collectives: 43.8 us -> 5.86 us
  local copies, waits for them, and re-layouts: 0.64 us -> 28.7 us
    pallas_call x0 -> x2, Pallas kernels: none -> 985 us  [the longest x1 832 us: backward(): pl.pallas_call(functools.partial(grad_kernel, blocks, base), grid=(blocks...]
    reduce_scatter x1 -> x0, waiting for transfers between devices: 943 us -> none  [device_fn(): grad_emb = lax.psum_scatter(emb_part, 'dp', scatter_dimension=1, tiled=True)]
    dot_general x3 -> x0, matrix products: 350 us -> none  [the longest x1 119 us: device_fn(): jnp.einsum('nv,nd->vd', d_raw, normed, preferred_element_type=jnp.float32)]
    reduce_sum x4 -> x2, other arithmetic: 87.9 us -> 0.65 us  [the longest x1 0.61 us: device_fn(): sums = jnp.stack([jnp.sum(mask_f32), jnp.sum(mask_f32 * kl_tok)])]
    psum x1 -> x0, waiting for transfers between devices: 72.8 us -> none  [device_fn(): lax.psum(jnp.dot(d_raw, emb_loc, preferred_element_type=jnp.float32), 'tp')]
    convert_element_type x2 -> x3, other arithmetic: 76.2 us -> 7.21 us  [the longest x1 5.23 us: device_fn(): normed = rms_norm(hid_loc.astype(jnp.float32), scale).astype(jnp.bfloat16)]
    psum x3 -> x0, blocking collectives: 38.8 us -> none  [the longest x1 16 us: device_fn(): tok_count = lax.psum(jnp.sum(mask_f32), 'dp')]
    unnamed x18 -> x4, local copies, waits for them, and re-layouts: 0.62 us -> 21.7 us
  transfers between devices with their start and end apart: 2 -> 0, of which waited for: 2 -> 0; matrix products, arithmetic and copies ran while one was open for 8% -> 0% of each run, Pallas kernels for 0% -> 0%
where the time goes in v1:
time: 1030 us
  Pallas kernels  985 us (96%)
  local copies, waits for them, and re-layouts  28.7 us (3%)
  other arithmetic  13.1 us (1%)
    pallas_call x1, Pallas kernels, backward(): pl.pallas_call(functools.partial(grad_kernel, blocks, base), grid=(blocks...  832 us
    pallas_call x1, Pallas kernels, forward_stats(): pl.pallas_call(functools.partial(stats_kernel, steps), grid=(steps,), out...  153 us
    unnamed x4, local copies, waits for them, and re-layouts  21.7 us

profile of v1, /device:TPU:0, one launch (start us, length us, event | category | flops | bytes accessed | tf_op | source)
XLA Modules:
  0.0 1033.3 jit_solution(3285007451218255346)
XLA Ops:
  0.6 0.7 convert_element_type.17
  1.3 3.1 fusion
  4.4 0.7 broadcast_add_fusion
  5.1 1.3 convert_element_type.15
  6.4 5.2 fusion.2.g_ref
  11.6 0.0 copy-start
  11.6 152.6 %fwd_stats.1 = f32[4,1024,128]{2,1,0:T(8,128)} custom-call(bf16[1024,2048]{1,0:T(8,128)(2,1)} %fusion.2.g_ref, bf16[24576,2048]{1,0:T(8,128)(2,1)} %ex_ref.1, bf16[1024,24576]{1,0:T(8,128)(2,1)} %tx_ref.1, bf16[1024,24576]{1,0:T(8,128)(2,1)} %tx_ref.1), custom_call_target="tpu_custom_call" | custom-call | flops 103079215104 | bytes 150994944 | tf_op jit(solution)/shard_map/fwd_stats/pallas_call | solution.py:80
  164.2 2.2 copy.13
  166.4 5.9 all-gather
  172.2 0.1 reduce.2
  172.4 0.0 copy-done
  172.4 0.6 convert_reduce_fusion
  173.1 1.4 fusion.8
  174.4 0.7 broadcast_in_dim.8.mine_ref
  175.1 1.6 broadcast_in_dim.7.row_ref
  176.7 832.3 %bwd_scatter.1 = (f32[24576,256]{1,0:T(8,128)}, bf16[1024,2048]{1,0:T(8,128)(2,1)}, f32[24,128]{1,0:T(8,128)}) custom-call(bf16[1024,2048]{1,0:T(8,128)(2,1)} %fusion.2.g_ref, bf16[1024,2048]{1,0:T(8,128)(2,1)} %x_ref.1, f32[1,2048]{1,0:T(1,128)} %bitcast.34, f32[3,1024,128]{2,1,0:T(8,128)} %broadcast_in_dim.7.row_ref, f32[8,128]{1,0:T(8,128)} %broadcast_in_dim.8.mine_ref, ...), custom_call_target="tpu_custom_call" | custom-call | flops 309237645312 | bytes 150994944 | tf_op jit(solution)/shard_map/bwd_scatter/pallas_call | solution.py:331
  1009.1 1.2 slice.27
  1010.2 1.3 slice_bitcast_fusion
  1011.5 4.8 copy.38
  1016.3 16.9 %copy.39 = f32[24576,256]{1,0:T(8,128)} copy(f32[24576,256]{1,0:T(8,128)} %get-tuple-element.29) | data formatting | bytes 50331648
  (5 shorter events, 0.1 us)
Async XLA Ops:
  11.6 160.8 %copy-start = (s32[1024]{0:T(1024)S(1)}, s32[1024]{0:T(1024)}, u32[]{:S(2)}) copy-start(s32[1024]{0:T(1024)} %param.9) | copy-start | bytes 12292
